TPU v7x, 32 devices: a whole 2x2x4 slice. The times are simulated.
32 devices in a mesh: panel: 4 (over x, core), tile: 8 (over z, y).
Axes of the slice: x: 2, y: 2, z: 4, core: 2. Of those that a mesh axis runs over, the one named last changes fastest.
Arguments:
- residual: float32 [4, 8, 16, 8, 128], P('panel', 'tile'), may hold values from -6 to 6
- inverse: bfloat16 [4, 8, 2, 576, 576], P('panel', 'tile'), may hold values from -1 to 2
- blend_weight: float32 [576], replicated, may hold values from 0.1 to 1.9
- seam_table: int32 [4, 4, 3], replicated, may hold values from -1 to 3, as said below
Outputs:
- correction: float32 [4, 8, 16, 8, 128], P('panel', 'tile')
Inputs may be any that keep to these rules, and one draw needn't show every extreme that they name: seam_table[p, e] holds the neighbour panel across edge e of panel p (or -1), a rotation r and a reversal v. Every panel has neighbours across exactly two opposite edges (0 and 2, or 1 and 3) and the entries -1, 0, 0 on the other two; the panels form one closed cycle and each panel's two neighbours differ. If edge e of p faces panel q, then edge c = (e + 2 + r) mod 4 of q faces p with rotation (-r) mod 4 and the same reversal v. At least one seam joins edge 0 of a panel to edge 0 of another, with rotation 2 and reversal 1.
All inputs are finite; a program needn't handle non-finite values.
Results may differ from a plain program's by a relative error of at most 0.0029.
Values may be sent and summed in bfloat16 or wider, within the bound.
A program may use at most 128 MiB of HBM per device.

v0:
```python
import jax
import jax.numpy as jnp
from jax import lax
from jax.sharding import PartitionSpec as P

PANELS = 4
TILE_ROWS = 2
SUB = 8
INTERSECTION = 8


def passed_along(block, axis, distance):
    devices = range(lax.axis_size(axis))
    route = [(i - distance, i) for i in devices if i - distance in devices]
    return lax.ppermute(block, axis, route)


def neighbours_in(first_part, second_part, stride):
    from_below = passed_along(first_part, "tile", stride)
    from_above = passed_along(second_part, "tile", -stride)
    return (from_below, from_above)


def neighbours_out(first_part, second_part, stride):
    to_above = passed_along(first_part, "tile", stride)
    to_below = passed_along(second_part, "tile", -stride)
    return (to_above, to_below)


def band_index(edge_id, row_count, col_count):
    margin = INTERSECTION
    if edge_id == 0:
        return (slice(None), slice(0, margin))
    if edge_id == 1:
        return (slice(0, margin), slice(None))
    if edge_id == 2:
        return (slice(None), slice(col_count - margin, col_count))
    return (slice(row_count - margin, row_count), slice(None))


def to_band(window, edge_id):
    if edge_id == 0:
        return jnp.transpose(window[::-1], (1, 0, 2))
    if edge_id == 1:
        return window[::-1]
    if edge_id == 2:
        return jnp.transpose(window, (1, 0, 2))
    return window


def from_band(region, edge_id):
    if edge_id == 0:
        return jnp.transpose(region, (1, 0, 2))[::-1]
    if edge_id == 1:
        return region[::-1]
    if edge_id == 2:
        return jnp.transpose(region, (1, 0, 2))
    return region


def into_cells(edge_part, edge_id):
    if edge_id == 0:
        return jnp.transpose(edge_part, (1, 0, 2))
    if edge_id == 1:
        return edge_part
    if edge_id == 2:
        return jnp.transpose(edge_part[::-1], (1, 0, 2))
    return edge_part[::-1]


def placed(band, offset, live_edge, length_all):
    blank_band = jnp.zeros((band.shape[0], length_all, band.shape[2]), jnp.float32)
    filled = lax.dynamic_update_slice_in_dim(blank_band, band, offset, 1)
    return jnp.where(live_edge, filled, jnp.zeros_like(filled))


def build_buffer(bands, offsets, live_edge, panel_side, extra):
    length_all = panel_side + 2 * extra
    return jnp.stack(
        [
            (
                placed(bands[2 * slot_id], offsets[2 * slot_id], live_edge[2 * slot_id], length_all)
                + placed(
                    bands[2 * slot_id + 1],
                    offsets[2 * slot_id + 1],
                    live_edge[2 * slot_id + 1],
                    length_all,
                )
            )[:, extra : extra + panel_side]
            for slot_id in range(2)
        ]
    )


def slot_info(seam_row, slot_id):
    first_entry = seam_row[2 * slot_id]
    second_entry = seam_row[2 * slot_id + 1]
    first_live = first_entry[0] >= 0
    chosen = jnp.where(first_live, first_entry, second_entry)
    edge_id = jnp.where(first_live, 2 * slot_id, 2 * slot_id + 1)
    facing = (edge_id + 2 + chosen[1]) % 4
    return (jnp.maximum(chosen[0], 0), facing // 2, chosen[2])


def outgoing_of(totals, slot_facts):
    blank_slot = jnp.zeros_like(totals[0])
    return jnp.stack(
        [
            jnp.where(
                slot_facts[0][0] == target,
                totals[0],
                jnp.where(slot_facts[1][0] == target, totals[1], blank_slot),
            )
            for target in range(PANELS)
        ]
    )


def picked_of(arrived_all, slot_facts):
    return jnp.stack(
        [
            lax.dynamic_index_in_dim(arrived_all, slot_facts[slot_id][0], 0, keepdims=False)
            for slot_id in range(2)
        ]
    )


def gathered_edges(bands, seam_row, tile_rows, tile_cols):
    height = bands[0].shape[1]
    width = bands[1].shape[1]
    longest = max(height, width)
    columns = bands[0].shape[2]
    pieces = []
    for slot_id in range(2):
        column_type = seam_row[2 * slot_id, 0] >= 0
        column_band = bands[2 * slot_id]
        row_band = jnp.pad(bands[2 * slot_id + 1], ((0, 0), (0, longest - width), (0, 0)))
        pieces.append(jnp.where(column_type, column_band, row_band))
    gathered = lax.all_gather(jnp.stack(pieces)[None], "tile", axis=0, tiled=True)
    grid = gathered.reshape(tile_rows, tile_cols, 2, INTERSECTION, longest, columns)
    totals = []
    for slot_id in range(2):
        column_type = seam_row[2 * slot_id, 0] >= 0
        grid_col = 0 if slot_id == 0 else tile_cols - 1
        grid_row = 0 if slot_id == 0 else tile_rows - 1
        down_column = grid[:, grid_col, slot_id, :, :height]
        down_column = jnp.transpose(down_column, (1, 0, 2, 3)).reshape(
            INTERSECTION, tile_rows * height, columns
        )
        along_row = grid[grid_row, :, slot_id, :, :width]
        along_row = jnp.transpose(along_row, (1, 0, 2, 3)).reshape(
            INTERSECTION, tile_cols * width, columns
        )
        totals.append(jnp.where(column_type, down_column, along_row))
    return jnp.stack(totals)


def cross(bands, seam_row, forward, offsets, live_edge, panel_side, tile_rows, tile_cols):
    extra = 0 if forward else INTERSECTION
    slot_facts = [slot_info(seam_row, slot_id) for slot_id in range(2)]
    if forward:
        totals = gathered_edges(bands, seam_row, tile_rows, tile_cols)
        arrived_all = lax.all_to_all(
            outgoing_of(totals, slot_facts), "panel", split_axis=0, concat_axis=0, tiled=True
        )
    else:
        buffer = build_buffer(bands, offsets, live_edge, panel_side, extra)
        totals = lax.psum(buffer, "tile")
        arrived_all = lax.all_to_all(
            outgoing_of(totals, slot_facts), "panel", split_axis=0, concat_axis=0, tiled=True
        )
    arrived = picked_of(arrived_all, slot_facts)
    return [
        jnp.where(slot_facts[slot_id][2] > 0, arrived[slot_id][:, ::-1], arrived[slot_id])
        for slot_id in range(2)
    ]


def patches(padded, block_rows, block_cols):
    columns = padded.shape[-1]
    blocked = padded.reshape(block_rows + 2, SUB, block_cols + 2, SUB, columns)
    pieces = [
        blocked[row_shift : row_shift + block_rows, :, col_shift : col_shift + block_cols]
        for row_shift in range(3)
        for col_shift in range(3)
    ]
    stacked = jnp.stack(pieces).reshape(3, 3, block_rows, SUB, block_cols, SUB, columns)
    stacked = jnp.transpose(stacked, (2, 4, 0, 3, 1, 5, 6))
    return stacked.reshape(block_rows, block_cols, 9 * SUB * SUB, columns)


def intersection_add(solved, block_rows, block_cols):
    columns = solved.shape[-1]
    shaped = solved.reshape(block_rows, block_cols, 3, SUB, 3, SUB, columns)
    summed = jnp.zeros((block_rows + 2, SUB, block_cols + 2, SUB, columns), jnp.float32)
    for row_shift in range(3):
        for col_shift in range(3):
            block_part = jnp.transpose(shaped[:, :, row_shift, :, col_shift], (0, 2, 1, 3, 4))
            summed = summed.at[
                row_shift : row_shift + block_rows, :, col_shift : col_shift + block_cols
            ].add(block_part)
    return summed.reshape((block_rows + 2) * SUB, (block_cols + 2) * SUB, columns)


def local(residual, inverse, blend_weight, seam_table):
    margin = INTERSECTION
    source = residual[0, 0].astype(jnp.bfloat16)
    height, tile_width, columns = source.shape
    tile_rows = TILE_ROWS
    tile_cols = lax.axis_size("tile") // TILE_ROWS
    tile_id = lax.axis_index("tile")
    row_pos = tile_id // tile_cols
    col_pos = tile_id % tile_cols
    seam_row = lax.dynamic_index_in_dim(seam_table, lax.axis_index("panel"), 0, keepdims=False)
    panel_side = tile_width * tile_cols
    on_edge = [col_pos == 0, row_pos == 0, col_pos == tile_cols - 1, row_pos == tile_rows - 1]
    live_edge = [on_edge[edge_id] & (seam_row[edge_id, 0] >= 0) for edge_id in range(4)]
    offsets = [row_pos * height, col_pos * tile_width, row_pos * height, col_pos * tile_width]
    lengths = [height, tile_width, height, tile_width]
    left_valid = col_pos > 0
    right_valid = col_pos < tile_cols - 1
    below_rows, above_rows = neighbours_in(source[height - margin :], source[:margin], tile_cols)
    row_ext = jnp.concatenate([below_rows, source, above_rows], 0)
    left_cols, right_cols = neighbours_in(row_ext, row_ext, 1)
    left_cols = jnp.where(left_valid, left_cols, jnp.zeros_like(left_cols))
    right_cols = jnp.where(right_valid, right_cols, jnp.zeros_like(right_cols))
    extended = jnp.concatenate([left_cols, row_ext, right_cols], 1)
    own_strips = [
        jnp.transpose(source, (1, 0, 2)),
        source[:margin],
        jnp.transpose(source[:, ::-1], (1, 0, 2)),
        source[height - margin :][::-1],
    ]
    arrived = cross(
        own_strips, seam_row, True, offsets, live_edge, panel_side, tile_rows, tile_cols
    )
    rows_ext, cols_ext = (extended.shape[0], extended.shape[1])
    for edge_id in range(4):
        widened = jnp.pad(arrived[edge_id // 2], ((0, 0), (margin, margin), (0, 0)))
        window = lax.dynamic_slice_in_dim(
            widened, offsets[edge_id], lengths[edge_id] + 2 * margin, 1
        )
        where_band = band_index(edge_id, rows_ext, cols_ext)
        fresh_band = jnp.where(live_edge[edge_id], to_band(window, edge_id), extended[where_band])
        extended = extended.at[where_band].set(fresh_band)
    sub_rows, sub_cols = (height // SUB, tile_width // SUB)
    local_patches = patches(extended, sub_rows, sub_cols).reshape(
        sub_rows * sub_cols, 9 * SUB * SUB, columns
    )
    solved = jnp.einsum(
        "noi,nir->nor", inverse[0, 0], local_patches, preferred_element_type=jnp.float32
    )
    solved = solved * blend_weight[None, :, None]
    spread = intersection_add(
        solved.reshape(sub_rows, sub_cols, 9 * SUB * SUB, columns), sub_rows, sub_cols
    )
    ghost_sets = [
        from_band(spread[band_index(edge_id, rows_ext, cols_ext)], edge_id) for edge_id in range(4)
    ]
    returned = cross(
        ghost_sets, seam_row, False, offsets, live_edge, panel_side, tile_rows, tile_cols
    )
    got_left, got_right = neighbours_out(spread[:, tile_width + margin :], spread[:, :margin], 1)
    spread = spread.at[:, margin : 2 * margin].add(jnp.where(left_valid, got_left, 0.0))
    spread = spread.at[:, tile_width : tile_width + margin].add(
        jnp.where(right_valid, got_right, 0.0)
    )
    narrow = spread[:, margin : tile_width + margin]
    got_below, got_above = neighbours_out(narrow[height + margin :], narrow[:margin], tile_cols)
    narrow = narrow.at[margin : 2 * margin].add(got_below)
    narrow = narrow.at[height : height + margin].add(got_above)
    owned_cells = narrow[margin : height + margin]
    for edge_id in range(4):
        edge_part = lax.dynamic_slice_in_dim(
            returned[edge_id // 2], offsets[edge_id], lengths[edge_id], 1
        )
        where_cells = band_index(edge_id, height, tile_width)
        addition = jnp.where(live_edge[edge_id], into_cells(edge_part, edge_id), 0.0)
        owned_cells = owned_cells.at[where_cells].add(addition)
    return owned_cells[None, None]


def solution(mesh):
    placed = (P("panel", "tile", None, None, None), P("panel", "tile", None, None, None), P(), P())
    return jax.shard_map(
        local,
        mesh=mesh,
        in_specs=placed,
        out_specs=P("panel", "tile", None, None, None),
        check_vma=False,
    )
```

profile of v0, /device:TPU:0, one launch (start us, length us, event | category | flops | bytes accessed | tf_op | source)
XLA Modules:
  0.0 179.4 jit_solution(4141283619340578663)
XLA Ops:
  6.5 1.0 convert_element_type.14
  7.5 1.3 collective-permute-start.1
  8.8 6.0 %collective-permute-start = (bf16[8,8,128]{2,1,0:T(8,128)(2,1)S(1)}, bf16[8,8,128]{2,1,0:T(8,128)(2,1)S(1)}, u32[]{:S(2)}, u32[]{:S(2)}) collective-permute-start(bf16[8,8,128]{2,1,0:T(8,128)(2,1)S(1)} %get-tuple-element.301), channel_id=1, source_target_pairs={{0,4},{1,5},{2,6},{3,7},{8,12},{9,13},{10,14},{11,15},{16,20},{17,... | collective-permute-start | bytes 49160 | tf_op jit(solution)/shard_map/ppermute | solution.py:15
  14.8 0.8 convert_bitcast_fusion.1
  15.6 0.8 convert_bitcast_fusion
  16.5 0.7 constant_dynamic-slice_fusion.8
  19.3 31.4 %all-gather = bf16[16,8,16,128]{3,2,1,0:T(8,128)(2,1)S(1)} all-gather(bf16[2,8,16,128]{3,2,1,0:T(8,128)(2,1)S(1)} %pad_maximum_fusion.5), channel_id=2, replica_groups=mesh['panel'=4,'tile'=8] {'tile'}, dimensions={0}, use_global_device_ids=true | all-gather | bytes 589824 | tf_op jit(solution)/shard_map/all_gather | solution.py:139
  50.8 0.7 constant_dynamic-slice_fusion.1
  54.7 0.7 pad_maximum_fusion.1
  55.5 3.6 %all-to-all-start = ((bf16[4,8,32,128]{3,2,1,0:T(8,128)(2,1)}), bf16[4,8,32,128]{3,2,1,0:T(8,128)(2,1)S(1)}, u32[]{:S(2)}, u32[]{:S(2)}) async-start(bf16[4,8,32,128]{3,2,1,0:T(8,128)(2,1)} %pad_maximum_fusion.1), calls=%async_computation | async-start | bytes 524288 | tf_op jit(solution)/shard_map/all_to_all | solution.py:163
  59.1 0.6 fusion.54
  62.9 1.3 concatenate.55
  64.2 0.8 concatenate.54
  65.0 1.3 collective-permute-start.3
  66.3 0.6 and_reduce_fusion
  66.9 4.5 %collective-permute-start.2 = (bf16[32,8,128]{2,1,0:T(8,128)(2,1)S(1)}, bf16[32,8,128]{2,1,0:T(8,128)(2,1)S(1)}, u32[]{:S(2)}, u32[]{:S(2)}) collective-permute-start(bf16[32,8,128]{2,1,0:T(8,128)(2,1)S(1)} %pad_maximum_fusion.4), channel_id=1, source_target_pairs={{0,1},{1,2},{2,3},{3,4},{4,5},{5,6},{6,7},{8,9},{9,10},{10,11},{11... | collective-permute-start | bytes 196616 | tf_op jit(solution)/shard_map/ppermute | solution.py:15
  71.5 1.9 %collective-permute-done.2 = bf16[32,8,128]{2,1,0:T(8,128)(2,1)S(1)} collective-permute-done((bf16[32,8,128]{2,1,0:T(8,128)(2,1)S(1)}, bf16[32,8,128]{2,1,0:T(8,128)(2,1)S(1)}, u32[]{:S(2)}, u32[]{:S(2)}) %collective-permute-start.2) | collective-permute-done | bytes 65568 | tf_op jit(solution)/shard_map/ppermute | solution.py:15
  74.8 1.3 fusion.7
  76.1 1.8 %fusion.8 = f32[4,8,3,8,128]{4,3,1,0,2:T(8,128)S(1)} fusion(f32[4,8,3,8,128]{4,3,1,0,2:T(8,128)S(1)} %fusion.7, s32[]{:T(128)} %bitcast.56, s32[]{:T(128)} %bitcast.57, f32[2,1,3,8,3,8,128]{6,5,4,3,2,0,1:T(8,128)S(1)} %bitcast.226, pred[]{:T(512)} %get-tuple-element.273), kind=kLoop, calls=%fused_computation.33 | loop fusion | flops 32768 | bytes 196617 | tf_op jit(solution)/shard_map/scatter-add | solution.py:201
  78.2 1.3 collective-permute-start.5
  79.5 4.9 %collective-permute-start.4 = (f32[32,8,128]{2,1,0:T(8,128)S(1)}, f32[32,8,128]{2,1,0:T(8,128)S(1)}, u32[]{:S(2)}, u32[]{:S(2)}) collective-permute-start(f32[32,8,128]{2,1,0:T(8,128)S(1)} %get-tuple-element.289), channel_id=1, source_target_pairs={{0,1},{1,2},{2,3},{3,4},{4,5},{5,6},{6,7},{8,9},{9,10},{10,11},{11... | collective-permute-start | bytes 393224 | tf_op jit(solution)/shard_map/ppermute | solution.py:15
  84.7 0.7 pad_maximum_fusion.2
  85.4 2.7 %collective-permute-done.4 = f32[32,8,128]{2,1,0:T(8,128)S(1)} collective-permute-done((f32[32,8,128]{2,1,0:T(8,128)S(1)}, f32[32,8,128]{2,1,0:T(8,128)S(1)}, u32[]{:S(2)}, u32[]{:S(2)}) %collective-permute-start.4) | collective-permute-done | bytes 131104 | tf_op jit(solution)/shard_map/ppermute | solution.py:15
  88.2 4.1 %collective-permute-start.6 = (f32[8,8,128]{2,1,0:T(8,128)S(1)}, f32[8,8,128]{2,1,0:T(8,128)S(1)}, u32[]{:S(2)}, u32[]{:S(2)}) collective-permute-start(f32[8,8,128]{2,1,0:T(8,128)S(1)} %slice.940), channel_id=1, source_target_pairs={{0,4},{1,5},{2,6},{3,7},{8,12},{9,13},{10,14},{11,15},{16,20},{17,... | collective-permute-start | bytes 98312 | tf_op jit(solution)/shard_map/ppermute | solution.py:15
  92.2 64.6 %all-reduce.7.cloned.1.call-done = f32[2,8,32,128]{3,2,1,0:T(8,128)} async-done(((f32[2,8,32,128]{3,2,1,0:T(8,128)}), f32[2,8,32,128]{3,2,1,0:T(8,128)}) %all-reduce.7.cloned.1.call-update) | async-done | bytes 262160 | tf_op jit(solution)/shard_map/psum | solution.py:168
  156.9 1.0 select_select_fusion.3
  157.9 0.9 pad_maximum_fusion
  158.7 3.5 %all-to-all-start.1 = ((f32[4,8,32,128]{3,2,1,0:T(8,128)}), f32[4,8,32,128]{3,2,1,0:T(8,128)S(1)}, u32[]{:S(2)}, u32[]{:S(2)}) async-start(f32[4,8,32,128]{3,2,1,0:T(8,128)} %pad_maximum_fusion), calls=%async_computation.1 | async-start | bytes 1048576 | tf_op jit(solution)/shard_map/all_to_all | solution.py:169
  162.3 1.3 collective-permute-start.7
  163.6 6.0 %collective-permute-done.7 = f32[8,8,128]{2,1,0:T(8,128)S(1)} collective-permute-done((f32[8,8,128]{2,1,0:T(8,128)S(1)}, f32[8,8,128]{2,1,0:T(8,128)S(1)}, u32[]{:S(2)}, u32[]{:S(2)}) %collective-permute-start.7) | collective-permute-done | bytes 32800 | tf_op jit(solution)/shard_map/ppermute | solution.py:15
  169.6 1.4 all-to-all-done.1
  171.3 0.6 copy.201
  (103 shorter events, 4.7 us)
Async XLA Ops:
  6.5 67.5 %copy-start = (bf16[1,1,2,576,576]{4,3,2,1,0:T(8,128)(2,1)S(1)}, bf16[1,1,2,576,576]{4,3,2,1,0:T(8,128)(2,1)}, u32[]{:S(2)}) copy-start(bf16[1,1,2,576,576]{4,3,2,1,0:T(8,128)(2,1)} %param.51) | copy-start | bytes 3981316
  6.5 44.2 %copy-start.1 = (s32[4,4,3]{1,0,2:T(4,128)S(1)}, s32[4,4,3]{1,0,2:T(4,128)}, u32[]{:S(2)}) copy-start(s32[4,4,3]{1,0,2:T(4,128)} %param.53) | copy-start | bytes 580
  7.5 57.4 %collective-permute-start.1 = (bf16[8,8,128]{2,1,0:T(8,128)(2,1)S(1)}, bf16[8,8,128]{2,1,0:T(8,128)(2,1)S(1)}, u32[]{:S(2)}, u32[]{:S(2)}) collective-permute-start(bf16[8,8,128]{2,1,0:T(8,128)(2,1)S(1)} %get-tuple-element.302), channel_id=1, source_target_pairs={{4,0},{5,1},{6,2},{7,3},{12,8},{13,9},{14,10},{15,11},{20,16},{21,... | collective-permute-start | bytes 49160 | tf_op jit(solution)/shard_map/ppermute | solution.py:15
  8.8 56.2 %collective-permute-start = (bf16[8,8,128]{2,1,0:T(8,128)(2,1)S(1)}, bf16[8,8,128]{2,1,0:T(8,128)(2,1)S(1)}, u32[]{:S(2)}, u32[]{:S(2)}) collective-permute-start(bf16[8,8,128]{2,1,0:T(8,128)(2,1)S(1)} %get-tuple-element.301), channel_id=1, source_target_pairs={{0,4},{1,5},{2,6},{3,7},{8,12},{9,13},{10,14},{11,15},{16,20},{17,... | collective-permute-start | bytes 49160 | tf_op jit(solution)/shard_map/ppermute | solution.py:15
  50.7 15.6 %copy-start.3 = (s32[5]{0:T(128)S(1)}, s32[5]{0:T(128)}, u32[]{:S(2)}) copy-start(s32[5]{0:T(128)} %constant.662.clone.1) | copy-start | bytes 64
  55.5 18.0 %all-to-all-start = ((bf16[4,8,32,128]{3,2,1,0:T(8,128)(2,1)}), bf16[4,8,32,128]{3,2,1,0:T(8,128)(2,1)S(1)}, u32[]{:S(2)}, u32[]{:S(2)}) async-start(bf16[4,8,32,128]{3,2,1,0:T(8,128)(2,1)} %pad_maximum_fusion.1), calls=%async_computation | async-start | bytes 524288 | tf_op jit(solution)/shard_map/all_to_all | solution.py:163
  59.1 97.7 %all-reduce.7.cloned.1.call-start = ((), (), s32[]{:S(2)}) async-start(), calls=%async_computation.2 | async-start | bytes 524288 | tf_op jit(solution)/shard_map/psum | solution.py:168
  65.0 6.5 %collective-permute-start.3 = (bf16[32,8,128]{2,1,0:T(8,128)(2,1)S(1)}, bf16[32,8,128]{2,1,0:T(8,128)(2,1)S(1)}, u32[]{:S(2)}, u32[]{:S(2)}) collective-permute-start(bf16[32,8,128]{2,1,0:T(8,128)(2,1)S(1)} %pad_maximum_fusion.4), channel_id=1, source_target_pairs={{1,0},{2,1},{3,2},{4,3},{5,4},{6,5},{7,6},{9,8},{10,9},{11,10},{12... | collective-permute-start | bytes 196616 | tf_op jit(solution)/shard_map/ppermute | solution.py:15
  66.9 6.4 %collective-permute-start.2 = (bf16[32,8,128]{2,1,0:T(8,128)(2,1)S(1)}, bf16[32,8,128]{2,1,0:T(8,128)(2,1)S(1)}, u32[]{:S(2)}, u32[]{:S(2)}) collective-permute-start(bf16[32,8,128]{2,1,0:T(8,128)(2,1)S(1)} %pad_maximum_fusion.4), channel_id=1, source_target_pairs={{0,1},{1,2},{2,3},{3,4},{4,5},{5,6},{6,7},{8,9},{9,10},{10,11},{11... | collective-permute-start | bytes 196616 | tf_op jit(solution)/shard_map/ppermute | solution.py:15
  73.5 0.7 copy-start.2
  78.2 7.2 %collective-permute-start.5 = (f32[32,8,128]{2,1,0:T(8,128)S(1)}, f32[32,8,128]{2,1,0:T(8,128)S(1)}, u32[]{:S(2)}, u32[]{:S(2)}) collective-permute-start(f32[32,8,128]{2,1,0:T(8,128)S(1)} %get-tuple-element.288), channel_id=1, source_target_pairs={{1,0},{2,1},{3,2},{4,3},{5,4},{6,5},{7,6},{9,8},{10,9},{11,10},{12... | collective-permute-start | bytes 393224 | tf_op jit(solution)/shard_map/ppermute | solution.py:15
  79.5 8.7 %collective-permute-start.4 = (f32[32,8,128]{2,1,0:T(8,128)S(1)}, f32[32,8,128]{2,1,0:T(8,128)S(1)}, u32[]{:S(2)}, u32[]{:S(2)}) collective-permute-start(f32[32,8,128]{2,1,0:T(8,128)S(1)} %get-tuple-element.289), channel_id=1, source_target_pairs={{0,1},{1,2},{2,3},{3,4},{4,5},{5,6},{6,7},{8,9},{9,10},{10,11},{11... | collective-permute-start | bytes 393224 | tf_op jit(solution)/shard_map/ppermute | solution.py:15
  88.2 74.1 %collective-permute-start.6 = (f32[8,8,128]{2,1,0:T(8,128)S(1)}, f32[8,8,128]{2,1,0:T(8,128)S(1)}, u32[]{:S(2)}, u32[]{:S(2)}) collective-permute-start(f32[8,8,128]{2,1,0:T(8,128)S(1)} %slice.940), channel_id=1, source_target_pairs={{0,4},{1,5},{2,6},{3,7},{8,12},{9,13},{10,14},{11,15},{16,20},{17,... | collective-permute-start | bytes 98312 | tf_op jit(solution)/shard_map/ppermute | solution.py:15
  158.7 12.3 %all-to-all-start.1 = ((f32[4,8,32,128]{3,2,1,0:T(8,128)}), f32[4,8,32,128]{3,2,1,0:T(8,128)S(1)}, u32[]{:S(2)}, u32[]{:S(2)}) async-start(f32[4,8,32,128]{3,2,1,0:T(8,128)} %pad_maximum_fusion), calls=%async_computation.1 | async-start | bytes 1048576 | tf_op jit(solution)/shard_map/all_to_all | solution.py:169
  162.3 7.3 %collective-permute-start.7 = (f32[8,8,128]{2,1,0:T(8,128)S(1)}, f32[8,8,128]{2,1,0:T(8,128)S(1)}, u32[]{:S(2)}, u32[]{:S(2)}) collective-permute-start(f32[8,8,128]{2,1,0:T(8,128)S(1)} %get-tuple-element.296), channel_id=1, source_target_pairs={{4,0},{5,1},{6,2},{7,3},{12,8},{13,9},{14,10},{15,11},{20,16},{21,... | collective-permute-start | bytes 98312 | tf_op jit(solution)/shard_map/ppermute | solution.py:15
Sparse Core Ops, SparseCore 0:
  85.5 71.2 all-reduce.6
where the time goes:
time: 180 us; the launch traced here: 179 us
  waiting for transfers between devices  76.6 us (43%)
  starting transfers between devices  31.7 us (18%)
  blocking collectives  31.4 us (17%)
  between operations  20.5 us (11%)
  other arithmetic  11.2 us (6%)
  local copies, waits for them, and re-layouts  7.37 us (4%)
    psum x1, waiting for transfers between devices, cross(): totals = lax.psum(buffer, 'tile')  64.6 us
    all_gather x1, blocking collectives, gathered_edges(): lax.all_gather(jnp.stack(pieces)[None], 'tile', axis=0, tiled=True)  31.4 us
    ppermute x8, starting transfers between devices, passed_along(): return lax.ppermute(block, axis, route)  24.6 us
    ppermute x8, waiting for transfers between devices, passed_along(): return lax.ppermute(block, axis, route)  10.6 us
    all_to_all x2, starting transfers between devices, cross(): lax.all_to_all(outgoing_of(totals, slot_facts), 'panel', split_axis=0, co...  7.11 us
  transfers between devices with their start and end apart: 11, of which 5 were waited for; matrix products, arithmetic and copies ran while one was open for 7% of the time, Pallas kernels for 0%

commit v1 on v0

--- a/solution.py
+++ b/solution.py
@@ -1,3 +1,4 @@
+import functools
 import jax
 import jax.numpy as jnp
 from jax import lax
@@ -7,6 +8,14 @@
 TILE_ROWS = 2
 SUB = 8
 INTERSECTION = 8
+
+
+def _answer_threads(q_in, mesh_name):
+    r2 = jnp.sum(lax.all_gather(q_in, mesh_name), 0)
+    return r2
+
+
+work_loads = functools.partial(_answer_threads, mesh_name="tile")
 
 
 def passed_along(block, axis, distance):
@@ -165,7 +174,7 @@
         )
     else:
         buffer = build_buffer(bands, offsets, live_edge, panel_side, extra)
-        totals = lax.psum(buffer, "tile")
+        totals = work_loads(buffer)
         arrived_all = lax.all_to_all(
             outgoing_of(totals, slot_facts), "panel", split_axis=0, concat_axis=0, tiled=True
         )

time: 180 us -> 151 us (0.84)
  waiting for transfers between devices: 76.6 us -> 51.8 us
  starting transfers between devices: 31.7 us -> 28.3 us
  other arithmetic: 11.2 us -> 8.27 us
  local copies, waits for them, and re-layouts: 7.37 us -> 9.44 us
    psum x1 -> x0, waiting for transfers between devices: 64.6 us -> none  [cross(): totals = lax.psum(buffer, 'tile')]
    all_gather x0 -> x1, waiting for transfers between devices: none -> 35.9 us  [_answer_threads(): r2 = jnp.sum(lax.all_gather(q_in, mesh_name), 0)]
    ppermute x8, starting transfers between devices: 24.6 us -> 21.2 us  [passed_along(): return lax.ppermute(block, axis, route)]
    ppermute x8, waiting for transfers between devices: 10.6 us -> 13.9 us  [passed_along(): return lax.ppermute(block, axis, route)]
    reduce_sum x0 -> x1, other arithmetic: none -> 1.82 us  [_answer_threads(): r2 = jnp.sum(lax.all_gather(q_in, mesh_name), 0)]
    convert_element_type x2 -> x0, other arithmetic: 1.82 us -> none  [local(): source = residual[0, 0].astype(jnp.bfloat16)]
  transfers between devices with their start and end apart: 11 -> 11, of which waited for: 5 -> 6; matrix products, arithmetic and copies ran while one was open for 7% -> 7% of each run, Pallas kernels for 0% -> 0%
where the time goes in v1:
time: 151 us; the launch traced here: 150 us
  waiting for transfers between devices  51.8 us (34%)
  blocking collectives  31.4 us (21%)
  starting transfers between devices  28.3 us (19%)
  between operations  20.6 us (14%)
  local copies, waits for them, and re-layouts  9.44 us (6%)
  other arithmetic  8.27 us (5%)
    all_gather x1, waiting for transfers between devices, _answer_threads(): r2 = jnp.sum(lax.all_gather(q_in, mesh_name), 0)  35.9 us
    all_gather x1, blocking collectives, gathered_edges(): lax.all_gather(jnp.stack(pieces)[None], 'tile', axis=0, tiled=True)  31.4 us
    ppermute x8, starting transfers between devices, passed_along(): return lax.ppermute(block, axis, route)  21.2 us
    ppermute x8, waiting for transfers between devices, passed_along(): return lax.ppermute(block, axis, route)  13.9 us
    all_to_all x2, starting transfers between devices, cross(): lax.all_to_all(outgoing_of(totals, slot_facts), 'panel', split_axis=0, co...  7.11 us
    another operation x8, local copies, waits for them, and re-layouts  3.42 us
    scatter-add x8, other arithmetic, intersection_add(): summed = summed.at[row_shift:row_shift + block_rows, :, col_shift:col_shi...  3.29 us
  transfers between devices with their start and end apart: 11, of which 6 were waited for; matrix products, arithmetic and copies ran while one was open for 7% of the time, Pallas kernels for 0%

profile of v1, /device:TPU:0, one launch (start us, length us, event | category | flops | bytes accessed | tf_op | source)
XLA Modules:
  0.0 150.4 jit_solution(12515410976228673449)
XLA Ops:
  6.5 1.0 copy.315
  7.5 1.3 collective-permute-start.1
  8.8 6.0 %collective-permute-start = (bf16[8,8,128]{2,0,1:T(8,128)(2,1)S(1)}, bf16[8,8,128]{2,0,1:T(8,128)(2,1)S(1)}, u32[]{:S(2)}, u32[]{:S(2)}) collective-permute-start(bf16[8,8,128]{2,0,1:T(8,128)(2,1)S(1)} %get-tuple-element.302), channel_id=1, source_target_pairs={{0,4},{1,5},{2,6},{3,7},{8,12},{9,13},{10,14},{11,15},{16,20},{17,... | collective-permute-start | bytes 49160 | tf_op jit(solution)/shard_map/ppermute | solution.py:24
  14.9 0.7 constant_dynamic-slice_fusion.8
  17.6 31.4 %all-gather = bf16[16,8,16,128]{3,2,1,0:T(8,128)(2,1)S(1)} all-gather(bf16[2,8,16,128]{3,2,1,0:T(8,128)(2,1)S(1)} %copy.216), channel_id=2, replica_groups=mesh['panel'=4,'tile'=8] {'tile'}, dimensions={0}, use_global_device_ids=true | all-gather | bytes 589824 | tf_op jit(solution)/shard_map/all_gather | solution.py:148
  49.1 0.6 constant_dynamic-slice_fusion.2
  53.2 0.7 pad_maximum_fusion.1
  53.9 3.6 %all-to-all-start = ((bf16[4,8,32,128]{3,1,2,0:T(8,128)(2,1)}), bf16[4,8,32,128]{3,1,2,0:T(8,128)(2,1)S(1)}, u32[]{:S(2)}, u32[]{:S(2)}) async-start(bf16[4,8,32,128]{3,1,2,0:T(8,128)(2,1)} %pad_maximum_fusion.1), calls=%async_computation | async-start | bytes 524288 | tf_op jit(solution)/shard_map/all_to_all | solution.py:172
  57.6 0.6 fusion.47
  60.7 0.6 slice.865
  61.4 1.3 concatenate.55
  62.7 0.8 concatenate.54
  63.5 1.3 collective-permute-start.3
  64.9 0.6 and_reduce_fusion
  65.5 4.5 %collective-permute-start.2 = (bf16[32,8,128]{2,1,0:T(8,128)(2,1)S(1)}, bf16[32,8,128]{2,1,0:T(8,128)(2,1)S(1)}, u32[]{:S(2)}, u32[]{:S(2)}) collective-permute-start(bf16[32,8,128]{2,1,0:T(8,128)(2,1)S(1)} %pad_maximum_fusion.4), channel_id=1, source_target_pairs={{0,1},{1,2},{2,3},{3,4},{4,5},{5,6},{6,7},{8,9},{9,10},{10,11},{11... | collective-permute-start | bytes 196616 | tf_op jit(solution)/shard_map/ppermute | solution.py:24
  70.1 1.9 %collective-permute-done.2 = bf16[32,8,128]{2,1,0:T(8,128)(2,1)S(1)} collective-permute-done((bf16[32,8,128]{2,1,0:T(8,128)(2,1)S(1)}, bf16[32,8,128]{2,1,0:T(8,128)(2,1)S(1)}, u32[]{:S(2)}, u32[]{:S(2)}) %collective-permute-start.2) | collective-permute-done | bytes 65568 | tf_op jit(solution)/shard_map/ppermute | solution.py:24
  73.4 1.3 fusion.6
  74.7 1.9 %fusion.7 = f32[4,8,3,8,128]{4,3,1,0,2:T(8,128)S(1)} fusion(f32[4,8,3,8,128]{4,3,1,0,2:T(8,128)S(1)} %fusion.6, s32[]{:T(128)} %bitcast.56, s32[]{:T(128)} %bitcast.57, f32[2,1,3,8,3,8,128]{6,5,4,3,2,0,1:T(8,128)S(1)} %bitcast.227, pred[]{:T(512)} %get-tuple-element.273), kind=kLoop, calls=%fused_computation.37 | loop fusion | flops 32768 | bytes 196617 | tf_op jit(solution)/shard_map/scatter-add | solution.py:210
  77.3 0.7 copy.256
  78.0 4.3 %collective-permute-start.4 = (f32[32,8,128]{2,1,0:T(8,128)S(1)}, f32[32,8,128]{2,1,0:T(8,128)S(1)}, u32[]{:S(2)}, u32[]{:S(2)}) collective-permute-start(f32[32,8,128]{2,1,0:T(8,128)S(1)} %get-tuple-element.288), channel_id=1, source_target_pairs={{0,1},{1,2},{2,3},{3,4},{4,5},{5,6},{6,7},{8,9},{9,10},{10,11},{11... | collective-permute-start | bytes 393224 | tf_op jit(solution)/shard_map/ppermute | solution.py:24
  82.3 1.3 collective-permute-start.5
  83.6 1.2 collective-permute-done.4
  84.8 5.4 %collective-permute-done.5 = f32[32,8,128]{2,1,0:T(8,128)S(1)} collective-permute-done((f32[32,8,128]{2,1,0:T(8,128)S(1)}, f32[32,8,128]{2,1,0:T(8,128)S(1)}, u32[]{:S(2)}, u32[]{:S(2)}) %collective-permute-start.5) | collective-permute-done | bytes 131104 | tf_op jit(solution)/shard_map/ppermute | solution.py:24
  90.3 1.3 collective-permute-start.6
  91.6 35.9 %all-gather.4.cloned.1.call-done = f32[16,8,32,128]{3,2,1,0:T(8,128)} async-done(((f32[2,8,32,128]{3,2,1,0:T(8,128)}), f32[16,8,32,128]{3,2,1,0:T(8,128)}) %all-gather.4.cloned.1.call-update) | async-done | bytes 2097168 | tf_op jit(solution)/shard_map/all_gather | solution.py:14
  127.5 1.8 %reduce_sum.9 = f32[2,8,32,128]{3,2,1,0:T(8,128)S(1)} reduce(f32[8,2,8,32,128]{4,3,2,1,0:T(8,128)} %bitcast.243, f32[]{:T(128)} %constant.660.clone.1), dimensions={0}, to_apply=%region_2.3 | reduce | flops 458752 | bytes 2359300 | tf_op jit(solution)/shard_map/reduce_sum | solution.py:14
  129.6 0.8 pad_maximum_fusion
  130.4 3.5 %all-to-all-start.1 = ((f32[4,8,32,128]{3,1,2,0:T(8,128)}), f32[4,8,32,128]{3,1,2,0:T(8,128)S(1)}, u32[]{:S(2)}, u32[]{:S(2)}) async-start(f32[4,8,32,128]{3,1,2,0:T(8,128)} %pad_maximum_fusion), calls=%async_computation.1 | async-start | bytes 1048576 | tf_op jit(solution)/shard_map/all_to_all | solution.py:178
  133.9 1.3 collective-permute-start.7
  135.2 5.4 %collective-permute-done.7 = f32[8,8,128]{2,0,1:T(8,128)S(1)} collective-permute-done((f32[8,8,128]{2,0,1:T(8,128)S(1)}, f32[8,8,128]{2,0,1:T(8,128)S(1)}, u32[]{:S(2)}, u32[]{:S(2)}) %collective-permute-start.7) | collective-permute-done | bytes 32800 | tf_op jit(solution)/shard_map/ppermute | solution.py:24
  140.6 2.0 %all-to-all-done.1 = f32[4,8,32,128]{3,1,2,0:T(8,128)S(1)} async-done(((f32[4,8,32,128]{3,1,2,0:T(8,128)}), f32[4,8,32,128]{3,1,2,0:T(8,128)S(1)}, u32[]{:S(2)}, u32[]{:S(2)}) %all-to-all-start.1) | async-done | bytes 524320 | tf_op jit(solution)/shard_map/all_to_all | solution.py:178
  142.9 0.7 copy.260
  (116 shorter events, 4.0 us)
Async XLA Ops:
  6.5 66.2 %copy-start = (bf16[1,1,2,576,576]{4,3,2,1,0:T(8,128)(2,1)S(1)}, bf16[1,1,2,576,576]{4,3,2,1,0:T(8,128)(2,1)}, u32[]{:S(2)}) copy-start(bf16[1,1,2,576,576]{4,3,2,1,0:T(8,128)(2,1)} %param.51) | copy-start | bytes 3981316
  6.5 42.6 %copy-start.1 = (s32[4,4,3]{1,0,2:T(4,128)S(1)}, s32[4,4,3]{1,0,2:T(4,128)}, u32[]{:S(2)}) copy-start(s32[4,4,3]{1,0,2:T(4,128)} %param.53) | copy-start | bytes 580
  7.5 56.0 %collective-permute-start.1 = (bf16[8,8,128]{2,0,1:T(8,128)(2,1)S(1)}, bf16[8,8,128]{2,0,1:T(8,128)(2,1)S(1)}, u32[]{:S(2)}, u32[]{:S(2)}) collective-permute-start(bf16[8,8,128]{2,0,1:T(8,128)(2,1)S(1)} %get-tuple-element.303), channel_id=1, source_target_pairs={{4,0},{5,1},{6,2},{7,3},{12,8},{13,9},{14,10},{15,11},{20,16},{21,... | collective-permute-start | bytes 49160 | tf_op jit(solution)/shard_map/ppermute | solution.py:24
  8.8 54.7 %collective-permute-start = (bf16[8,8,128]{2,0,1:T(8,128)(2,1)S(1)}, bf16[8,8,128]{2,0,1:T(8,128)(2,1)S(1)}, u32[]{:S(2)}, u32[]{:S(2)}) collective-permute-start(bf16[8,8,128]{2,0,1:T(8,128)(2,1)S(1)} %get-tuple-element.302), channel_id=1, source_target_pairs={{0,4},{1,5},{2,6},{3,7},{8,12},{9,13},{10,14},{11,15},{16,20},{17,... | collective-permute-start | bytes 49160 | tf_op jit(solution)/shard_map/ppermute | solution.py:24
  49.1 15.7 %copy-start.3 = (s32[5]{0:T(128)S(1)}, s32[5]{0:T(128)}, u32[]{:S(2)}) copy-start(s32[5]{0:T(128)} %constant.662.clone.1) | copy-start | bytes 64
  53.9 18.1 %all-to-all-start = ((bf16[4,8,32,128]{3,1,2,0:T(8,128)(2,1)}), bf16[4,8,32,128]{3,1,2,0:T(8,128)(2,1)S(1)}, u32[]{:S(2)}, u32[]{:S(2)}) async-start(bf16[4,8,32,128]{3,1,2,0:T(8,128)(2,1)} %pad_maximum_fusion.1), calls=%async_computation | async-start | bytes 524288 | tf_op jit(solution)/shard_map/all_to_all | solution.py:172
  57.6 70.0 %all-gather.4.cloned.1.call-start = ((), (), s32[]{:S(2)}) async-start(), calls=%async_computation.2 | async-start | bytes 2359296 | tf_op jit(solution)/shard_map/all_gather | solution.py:14
  63.5 6.5 %collective-permute-start.3 = (bf16[32,8,128]{2,1,0:T(8,128)(2,1)S(1)}, bf16[32,8,128]{2,1,0:T(8,128)(2,1)S(1)}, u32[]{:S(2)}, u32[]{:S(2)}) collective-permute-start(bf16[32,8,128]{2,1,0:T(8,128)(2,1)S(1)} %pad_maximum_fusion.4), channel_id=1, source_target_pairs={{1,0},{2,1},{3,2},{4,3},{5,4},{6,5},{7,6},{9,8},{10,9},{11,10},{12... | collective-permute-start | bytes 196616 | tf_op jit(solution)/shard_map/ppermute | solution.py:24
  65.5 6.4 %collective-permute-start.2 = (bf16[32,8,128]{2,1,0:T(8,128)(2,1)S(1)}, bf16[32,8,128]{2,1,0:T(8,128)(2,1)S(1)}, u32[]{:S(2)}, u32[]{:S(2)}) collective-permute-start(bf16[32,8,128]{2,1,0:T(8,128)(2,1)S(1)} %pad_maximum_fusion.4), channel_id=1, source_target_pairs={{0,1},{1,2},{2,3},{3,4},{4,5},{5,6},{6,7},{8,9},{9,10},{10,11},{11... | collective-permute-start | bytes 196616 | tf_op jit(solution)/shard_map/ppermute | solution.py:24
  72.1 0.7 copy-start.2
  78.0 6.8 %collective-permute-start.4 = (f32[32,8,128]{2,1,0:T(8,128)S(1)}, f32[32,8,128]{2,1,0:T(8,128)S(1)}, u32[]{:S(2)}, u32[]{:S(2)}) collective-permute-start(f32[32,8,128]{2,1,0:T(8,128)S(1)} %get-tuple-element.288), channel_id=1, source_target_pairs={{0,1},{1,2},{2,3},{3,4},{4,5},{5,6},{6,7},{8,9},{9,10},{10,11},{11... | collective-permute-start | bytes 393224 | tf_op jit(solution)/shard_map/ppermute | solution.py:24
  82.3 7.9 %collective-permute-start.5 = (f32[32,8,128]{2,1,0:T(8,128)S(1)}, f32[32,8,128]{2,1,0:T(8,128)S(1)}, u32[]{:S(2)}, u32[]{:S(2)}) collective-permute-start(f32[32,8,128]{2,1,0:T(8,128)S(1)} %get-tuple-element.287), channel_id=1, source_target_pairs={{1,0},{2,1},{3,2},{4,3},{5,4},{6,5},{7,6},{9,8},{10,9},{11,10},{12... | collective-permute-start | bytes 393224 | tf_op jit(solution)/shard_map/ppermute | solution.py:24
  90.3 43.5 %collective-permute-start.6 = (f32[8,8,128]{2,0,1:T(8,128)S(1)}, f32[8,8,128]{2,0,1:T(8,128)S(1)}, u32[]{:S(2)}, u32[]{:S(2)}) collective-permute-start(f32[8,8,128]{2,0,1:T(8,128)S(1)} %slice.940), channel_id=1, source_target_pairs={{0,4},{1,5},{2,6},{3,7},{8,12},{9,13},{10,14},{11,15},{16,20},{17,... | collective-permute-start | bytes 98312 | tf_op jit(solution)/shard_map/ppermute | solution.py:24
  130.4 12.3 %all-to-all-start.1 = ((f32[4,8,32,128]{3,1,2,0:T(8,128)}), f32[4,8,32,128]{3,1,2,0:T(8,128)S(1)}, u32[]{:S(2)}, u32[]{:S(2)}) async-start(f32[4,8,32,128]{3,1,2,0:T(8,128)} %pad_maximum_fusion), calls=%async_computation.1 | async-start | bytes 1048576 | tf_op jit(solution)/shard_map/all_to_all | solution.py:178
  133.9 6.7 %collective-permute-start.7 = (f32[8,8,128]{2,0,1:T(8,128)S(1)}, f32[8,8,128]{2,0,1:T(8,128)S(1)}, u32[]{:S(2)}, u32[]{:S(2)}) collective-permute-start(f32[8,8,128]{2,0,1:T(8,128)S(1)} %get-tuple-element.297), channel_id=1, source_target_pairs={{4,0},{5,1},{6,2},{7,3},{12,8},{13,9},{14,10},{15,11},{20,16},{21,... | collective-permute-start | bytes 98312 | tf_op jit(solution)/shard_map/ppermute | solution.py:24
Sparse Core Ops, SparseCore 0:
  78.2 49.3 all-gather.3
